TPU v7x, 32 devices: a 4x2x2 block of a 4x4x8 slice. The times are simulated.
32 devices in a mesh: mat: 4 (over y, z), row: 8 (over x, core).
Axes of the slice: x: 4, y: 2, z: 2, core: 2. Of those that a mesh axis runs over, the one named last changes fastest.
The devices are a block of a 4x4x8 slice.
Arguments:
- operand: bfloat16 [8192, 16384], P(('mat', 'row')), parts along dimension 0
Outputs:
- output 1: float32 [32, 5, 256, 256], P(('mat', 'row')), parts along dimension 0
- output 2: float32 [8192, 16384], P(('mat', 'row')), parts along dimension 0
There are 4 independent parts. A program takes and returns all parts, laid end to end along the dimension named above; each array names one.
All inputs are finite; a program needn't handle non-finite values.
Results may differ from a plain program's by a relative error of at most 0.001.
Values are sent between devices in bfloat16 or wider.
A program may use at most 768 MiB of HBM per device.

v0:
```python
import math
import jax
import jax.numpy as jnp
from jax import lax
from jax.sharding import PartitionSpec as P


def split_counts(groups):
    half_count = groups // 2
    low_count = 2 ** (int(math.log2(half_count)) // 2)
    return half_count, low_count, half_count // low_count


def solution(mesh):
    groups = mesh.shape["row"]
    half_count, low_count, high_count = split_counts(groups)
    low_offsets = [low_count - 1 - position for position in range(low_count)]
    high_offsets = [(position + 1) * low_count for position in range(high_count)]
    slot_shift = [low_count - 1 - position for lead_pos in range(high_count) for position in range(low_count)]

    def pull_from(tile_in, offset):
        if offset == 0:
            return tile_in
        return lax.ppermute(tile_in, "row", [((target + offset) % groups, target) for target in range(groups)])

    def push_to(tile_in, offset):
        return lax.ppermute(tile_in, "row", [(source, (source + offset) % groups) for source in range(groups)])

    def per_device(own_block):
        device = lax.axis_index("row")
        block_rows = own_block.shape[0]
        low_stack = jnp.stack([pull_from(own_block, offset) for offset in low_offsets])
        high_stack = jnp.stack([pull_from(own_block, offset) for offset in high_offsets])
        diag_block = jnp.einsum("bk,ck->bc", own_block, own_block, preferred_element_type=jnp.float32)
        cross_prod = jnp.einsum("jck,ybk->jycb", high_stack, low_stack, preferred_element_type=jnp.float32)
        flat_cross = cross_prod.reshape(half_count, block_rows, block_rows)
        distance = jnp.arange(1, half_count + 1)
        first_blk = (device + jnp.array(slot_shift, jnp.int32)) % groups
        wrapped = (first_blk + distance >= groups)[:, None, None]
        padded = ((distance == half_count) & (first_blk >= half_count))[:, None, None]
        oriented = jnp.where(wrapped, jnp.swapaxes(flat_cross, 1, 2), flat_cross)
        oriented = jnp.where(padded, 0.0, oriented)
        gram_local = jnp.concatenate([diag_block[None], oriented], axis=0)[None]
        cross_bf = jnp.where(padded, 0.0, flat_cross).astype(jnp.bfloat16).reshape(high_count, low_count, block_rows, block_rows)
        to_high = jnp.einsum("jycb,ybk->jck", cross_bf, low_stack, preferred_element_type=jnp.float32)
        to_low = jnp.einsum("jycb,jck->ybk", cross_bf, high_stack, preferred_element_type=jnp.float32)
        applied = to_low[low_count - 1] + jnp.dot(diag_block.astype(jnp.bfloat16), own_block, preferred_element_type=jnp.float32)
        for position in range(low_count - 1):
            applied = applied + push_to(to_low[position], low_offsets[position])
        for position in range(high_count):
            applied = applied + push_to(to_high[position], high_offsets[position])
        return gram_local, applied

    spec_rows = P(("mat", "row"), None)
    spec_slots = P(("mat", "row"), None, None, None)
    return jax.shard_map(per_device, mesh=mesh, in_specs=(spec_rows,), out_specs=(spec_slots, spec_rows), check_vma=False)
```

profile of v0, /device:TPU:80, one launch (start us, length us, event | category | flops | bytes accessed | tf_op | source)
XLA Modules:
  0.0 1372.1 jit_solution(1302974567445651194)
XLA Ops:
  0.6 2.1 collective-permute-start
  2.8 0.7 collective-permute-start.1
  3.4 0.4 collective-permute-start.2
  3.9 0.7 compare_and_fusion
  4.6 0.1 broadcast_in_dim.43
  4.6 0.1 copy.9
  4.8 179.8 %collective-permute-done = bf16[256,16384]{1,0:T(8,128)(2,1)} collective-permute-done((bf16[256,16384]{1,0:T(8,128)(2,1)}, bf16[256,16384]{1,0:T(8,128)(2,1)}, u32[]{:S(2)}, u32[]{:S(2)}) %collective-permute-start) | collective-permute-done | bytes 8388640 | tf_op jit(solution)/shard_map/ppermute | solution.py:24
  184.6 448.8 %collective-permute-done.1 = bf16[256,16384]{1,0:T(8,128)(2,1)} collective-permute-done((bf16[256,16384]{1,0:T(8,128)(2,1)}, bf16[256,16384]{1,0:T(8,128)(2,1)}, u32[]{:S(2)}, u32[]{:S(2)}) %collective-permute-start.1) | collective-permute-done | bytes 8388640 | tf_op jit(solution)/shard_map/ppermute | solution.py:24
  633.4 0.0 collective-permute-done.2
  633.4 14.3 %fusion.4 = f32[2,2,256,256]{2,3,0,1:T(8,128)S(1)} fusion(bf16[1,256,16384]{2,1,0:T(8,128)(2,1)} %bitcast.6, bf16[1,256,16384]{2,1,0:T(8,128)(2,1)} %bitcast.5, bf16[1,256,16384]{2,1,0:T(8,128)(2,1)} %bitcast.47, bf16[1,256,16384]{2,1,0:T(8,128)(2,1)} %bitcast.1), kind=kOutput, calls=%fused_computation.13 | convolution fusion | flops 8657043456 | bytes 34603008 | tf_op jit(solution)/shard_map/jck,ybk->jycb/dot_general | solution.py:35
  647.6 18.8 %convolution_bitcast_fusion = f32[2,256,16384]{2,1,0:T(8,128)} fusion(bf16[1,256,16384]{2,1,0:T(8,128)(2,1)} %bitcast.48, bf16[1,256,16384]{2,1,0:T(8,128)(2,1)} %bitcast.1, f32[2,2,256,256]{2,3,0,1:T(8,128)S(1)} %fusion.4, pred[2,2]{0,1:T(4,128)(4,1)S(1)} %copy.9), kind=kOutput, calls=%fused_computation | convolution fusion | flops 8598585344 | bytes 51380228 | tf_op jit(solution)/shard_map/jycb,ybk->jck/dot_general | solution.py:45
  666.5 18.8 %convolution_bitcast_fusion.1 = f32[2,256,16384]{2,1,0:T(8,128)} fusion(bf16[1,256,16384]{2,1,0:T(8,128)(2,1)} %bitcast.6, bf16[1,256,16384]{2,1,0:T(8,128)(2,1)} %bitcast.5, f32[2,2,256,256]{2,3,0,1:T(8,128)S(1)} %fusion.4, pred[2,2]{0,1:T(4,128)(4,1)S(1)} %copy.9), kind=kOutput, calls=%fused_computation.1 | convolution fusion | flops 8598585344 | bytes 51380228 | tf_op jit(solution)/shard_map/jycb,jck->ybk/dot_general | solution.py:46
  685.3 21.8 %slice_bitcast_fusion.1 = (f32[256,16384]{1,0:T(8,128)}, f32[256,16384]{1,0:T(8,128)}) fusion(f32[2,256,16384]{2,1,0:T(8,128)} %convolution_bitcast_fusion), kind=kLoop, calls=%fused_computation.7 | loop fusion | bytes 67108864 | tf_op jit(solution)/shard_map/squeeze | solution.py:51
  707.1 0.0 collective-permute-start.4
  707.1 0.0 slice-start
  707.1 0.0 slice-start.1
  707.1 5.2 collective-permute-start.5
  712.2 11.3 slice_bitcast_fusion.2
  723.5 0.0 collective-permute-start.3
  723.5 0.0 slice-done
  723.6 0.0 slice-done.1
  723.6 2.4 fusion.13
  725.9 0.3 copy.7
  726.3 0.3 copy.8
  726.6 0.2 fusion.5
  726.8 1.2 maximum_bitcast_fusion.10
  728.0 506.0 %collective-permute-done.4 = f32[256,16384]{1,0:T(8,128)} collective-permute-done((f32[256,16384]{1,0:T(8,128)}, f32[256,16384]{1,0:T(8,128)}, u32[]{:S(2)}, u32[]{:S(2)}) %collective-permute-start.4) | collective-permute-done | bytes 16777248 | tf_op jit(solution)/shard_map/ppermute | solution.py:27
  1234.0 106.9 %collective-permute-done.5 = f32[256,16384]{1,0:T(8,128)} collective-permute-done((f32[256,16384]{1,0:T(8,128)}, f32[256,16384]{1,0:T(8,128)}, u32[]{:S(2)}, u32[]{:S(2)}) %collective-permute-start.5) | collective-permute-done | bytes 16777248 | tf_op jit(solution)/shard_map/ppermute | solution.py:27
  1340.8 0.0 collective-permute-done.3
  1340.8 31.3 %fusion.2 = f32[256,16384]{1,0:T(8,128)} fusion(f32[256,16384]{1,0:T(8,128)} %collective-permute-done.5, f32[256,16384]{1,0:T(8,128)} %collective-permute-done.4, f32[256,16384]{1,0:T(8,128)} %collective-permute-done.3, bf16[256,16384]{1,0:T(8,128)(2,1)} %param.2, f32[2,256,16384]{2,1,0:T(8,128)} %convolution_bitcast_fusion.1, f32[256,256]{1,0:T(8,128)S(1)} %fusion.13), kind=kOutput, calls=%fused_computation.5 | convolution fusion | flops 2164326400 | bytes 92536832 | tf_op jit(solution)/shard_map/dot_general | solution.py:47
  (2 shorter events, 0.0 us)
Async XLA Ops:
  0.6 184.0 %collective-permute-start = (bf16[256,16384]{1,0:T(8,128)(2,1)}, bf16[256,16384]{1,0:T(8,128)(2,1)}, u32[]{:S(2)}, u32[]{:S(2)}) collective-permute-start(bf16[256,16384]{1,0:T(8,128)(2,1)} %param.2), channel_id=1, source_target_pairs={{1,0},{2,1},{3,2},{4,3},{5,4},{6,5},{7,6},{0,7},{9,8},{10,9},{11,1... | collective-permute-start | bytes 25165832 | tf_op jit(solution)/shard_map/ppermute | solution.py:24
  2.8 630.6 %collective-permute-start.1 = (bf16[256,16384]{1,0:T(8,128)(2,1)}, bf16[256,16384]{1,0:T(8,128)(2,1)}, u32[]{:S(2)}, u32[]{:S(2)}) collective-permute-start(bf16[256,16384]{1,0:T(8,128)(2,1)} %param.2), channel_id=1, source_target_pairs={{2,0},{3,1},{4,2},{5,3},{6,4},{7,5},{0,6},{1,7},{10,8},{11,9},{12,... | collective-permute-start | bytes 25165832 | tf_op jit(solution)/shard_map/ppermute | solution.py:24
  3.4 629.9 %collective-permute-start.2 = (bf16[256,16384]{1,0:T(8,128)(2,1)}, bf16[256,16384]{1,0:T(8,128)(2,1)}, u32[]{:S(2)}, u32[]{:S(2)}) collective-permute-start(bf16[256,16384]{1,0:T(8,128)(2,1)} %param.2), channel_id=1, source_target_pairs={{4,0},{5,1},{6,2},{7,3},{0,4},{1,5},{2,6},{3,7},{12,8},{13,9},{14,... | collective-permute-start | bytes 25165832 | tf_op jit(solution)/shard_map/ppermute | solution.py:24
  707.1 526.9 %collective-permute-start.4 = (f32[256,16384]{1,0:T(8,128)}, f32[256,16384]{1,0:T(8,128)}, u32[]{:S(2)}, u32[]{:S(2)}) collective-permute-start(f32[256,16384]{1,0:T(8,128)} %get-tuple-element.4), channel_id=1, source_target_pairs={{0,2},{1,3},{2,4},{3,5},{4,6},{5,7},{6,0},{7,1},{8,10},{9,11},{10,... | collective-permute-start | bytes 50331656 | tf_op jit(solution)/shard_map/ppermute | solution.py:27
  707.1 16.5 %slice-start = ((s8[8388608]{0:T(1024)(128)(4,1)}), s8[4194304]{0:T(1024)(128)(4,1)S(1)}, s32[]{:S(2)}) async-start(s8[8388608]{0:T(1024)(128)(4,1)} %bitcast.49), calls=%async_computation | async-start | bytes 8388608
  707.1 16.5 %slice-start.1 = ((s8[8388608]{0:T(1024)(128)(4,1)}), s8[4194304]{0:T(1024)(128)(4,1)S(1)}, s32[]{:S(2)}) async-start(s8[8388608]{0:T(1024)(128)(4,1)} %bitcast.49), calls=%async_computation.1 | async-start | bytes 8388608
  707.1 633.8 %collective-permute-start.5 = (f32[256,16384]{1,0:T(8,128)}, f32[256,16384]{1,0:T(8,128)}, u32[]{:S(2)}, u32[]{:S(2)}) collective-permute-start(f32[256,16384]{1,0:T(8,128)} %get-tuple-element.5), channel_id=1, source_target_pairs={{0,4},{1,5},{2,6},{3,7},{4,0},{5,1},{6,2},{7,3},{8,12},{9,13},{10,... | collective-permute-start | bytes 50331656 | tf_op jit(solution)/shard_map/ppermute | solution.py:27
  723.5 617.3 %collective-permute-start.3 = (f32[256,16384]{1,0:T(8,128)}, f32[256,16384]{1,0:T(8,128)}, u32[]{:S(2)}, u32[]{:S(2)}) collective-permute-start(f32[256,16384]{1,0:T(8,128)} %slice_bitcast_fusion.2), channel_id=1, source_target_pairs={{0,1},{1,2},{2,3},{3,4},{4,5},{5,6},{6,7},{7,0},{8,9},{9,10},{10,1... | collective-permute-start | bytes 50331656 | tf_op jit(solution)/shard_map/ppermute | solution.py:27
where the time goes:
time: 1370 us
  waiting for transfers between devices  1240 us (91%)
  matrix products  85.5 us (6%)
  local copies, waits for them, and re-layouts  34 us (2%)
    ppermute x3, waiting for transfers between devices, pull_from(): lax.ppermute(tile_in, 'row', [((target + offset) % groups, target) for ta...  629 us
    ppermute x3, waiting for transfers between devices, push_to(): lax.ppermute(tile_in, 'row', [(source, (source + offset) % groups) for so...  613 us
    dot_general x1, matrix products, per_device(): jnp.dot(diag_block.astype(jnp.bfloat16), own_block, preferred_element_typ...  31.3 us
  transfers between devices with their start and end apart: 6, of which 4 were waited for; matrix products, arithmetic and copies ran while one was open for 1% of the time, Pallas kernels for 0%

commit v1 on v0

v1 whole, which is shorter than its diff:
```python
import functools

import jax
import jax.numpy as jnp
from jax import lax
from jax.experimental import pallas as pl
from jax.experimental.pallas import tpu as pltpu
from jax.sharding import PartitionSpec as P

BATCHES = 4
GRAM_STEP = 2048
APPLY_STEP = 1024
OUT_PARTS = 8
VMEM_LIMIT = 67043328

NT = (((1,), (1,)), ((), ()))


def kernel(groups, a_ref, y_ref, g_ref, hb, own, work, far, acc, y_acc, x_gram,
           own_send, own_recv, fwd_send, fwd_recv, relay_send, relay_recv,
           far_send, far_recv, load_sem, out_sem):
    rows, cols = a_ref.shape
    half = rows // 2
    piece = half // BATCHES
    me = lax.axis_index("row")
    core = lax.rem(me, 2)
    right = lax.rem(me + 2, groups)
    left = lax.rem(me + groups - 2, groups)
    sib = me + 1 - 2 * core

    def remote(src, dst, send, recv, to):
        return pltpu.make_async_remote_copy(
            src_ref=src, dst_ref=dst, send_sem=send, recv_sem=recv,
            device_id={"row": to}, device_id_type=pl.DeviceIdType.MESH)

    barrier = pltpu.get_barrier_semaphore()
    for peer in (left, right, sib):
        pl.semaphore_signal(barrier, inc=1, device_id={"row": peer}, device_id_type=pl.DeviceIdType.MESH)
    pl.semaphore_wait(barrier, 3)

    def half_rows(index):
        return pl.ds(index * half, half)

    to_right = [remote(a_ref.at[half_rows(s)], hb.at[1, half_rows(s)], own_send.at[s], own_recv.at[s], right) for s in (0, 1)]
    to_left = [remote(a_ref.at[half_rows(s)], hb.at[2, half_rows(s)], own_send.at[2 + s], own_recv.at[2 + s], left) for s in (0, 1)]
    to_sib = remote(a_ref, hb.at[0], own_send.at[4], own_recv.at[4], sib)
    to_right[0].start()
    to_left[1].start()
    to_right[1].start()
    to_left[0].start()
    to_sib.start()

    fwd_right = [remote(hb.at[1, pl.ds(i * piece, piece)], far.at[i, pl.ds(0, piece)],
                        fwd_send.at[i], fwd_recv.at[i], right) for i in range(BATCHES)]
    fwd_left = [remote(hb.at[2, pl.ds(half + i * piece, piece)], far.at[i, pl.ds(piece, piece)],
                       fwd_send.at[BATCHES + i], fwd_recv.at[BATCHES + i], left) for i in range(BATCHES)]
    relay = [[remote(hb.at[1 + side, half_rows(s)], hb.at[3 + side, half_rows(s)],
                     relay_send.at[2 * side + s], relay_recv.at[2 * side + s], sib) for s in (0, 1)] for side in (0, 1)]
    far_relay = [remote(far.at[i, pl.ds(0, 2 * piece)], far.at[i, pl.ds(2 * piece, 2 * piece)],
                        far_send.at[i], far_recv.at[i], sib) for i in range(BATCHES)]

    def gram_t(left_ref, right_ref, count, base=0):
        acc[pl.ds(base, count), :] = jnp.zeros((count, rows), jnp.float32)

        def body(step, carry):
            sl = pl.ds(pl.multiple_of(step * GRAM_STEP, GRAM_STEP), GRAM_STEP)
            acc[pl.ds(base, count), :] += lax.dot_general(
                left_ref[:, sl], right_ref[:, sl], NT, preferred_element_type=jnp.float32)
            return carry

        lax.fori_loop(0, cols // GRAM_STEP, body, 0)

    def apply(b_ref, count, first=False):
        coef = acc[pl.ds(0, count), :].astype(jnp.bfloat16).T

        def body(step, carry):
            sl = pl.ds(pl.multiple_of(step * APPLY_STEP, APPLY_STEP), APPLY_STEP)
            term = jnp.dot(coef, b_ref[:, sl], preferred_element_type=jnp.float32)
            y_acc[:, sl] = term if first else y_acc[:, sl] + term
            return carry

        lax.fori_loop(0, cols // APPLY_STEP, body, 0)

    def oriented(value, slot):
        distance = slot
        shift = slot % 2
        first_blk = lax.rem(me + shift, groups)
        return jnp.where(first_blk + distance >= groups, value.T, value)

    def load(src, dst, sem):
        copy = pltpu.make_async_copy(src, dst, sem)
        copy.start()
        return copy

    first_load = load(a_ref, own, load_sem.at[0])
    first_load.wait()
    gram_t(own, own, rows)
    g_ref[0] = acc[pl.ds(0, rows), :]
    apply(own, rows, first=True)

    to_sib.wait_recv()
    load(hb.at[0], work.at[pl.ds(0, rows)], load_sem.at[1]).wait()
    gram_t(work.at[pl.ds(0, rows)], own, rows)
    apply(work.at[pl.ds(0, rows)], rows)

    to_right[0].wait_recv()
    for copy in fwd_right:
        copy.start()
    relay[0][0].start()
    to_left[1].wait_recv()
    for copy in fwd_left:
        copy.start()
    relay[1][1].start()
    to_right[1].wait_recv()
    relay[0][1].start()
    to_left[0].wait_recv()
    relay[1][0].start()

    for side in (0, 1):
        one = load(hb.at[1 + side], work.at[pl.ds(0, rows)], load_sem.at[2 + 2 * side])
        relay[side][0].wait_recv()
        relay[side][1].wait_recv()
        two = load(hb.at[3 + side], work.at[pl.ds(rows, rows)], load_sem.at[3 + 2 * side])
        one.wait()
        two.wait()
        gram_t(work, own, 2 * rows)
        if side == 1:
            g_ref[2] = oriented(acc[pl.ds(0, rows), :], 2)
        apply(work, 2 * rows)

    load(hb.at[4 * core], work.at[pl.ds(rows, rows)], load_sem.at[6]).wait()
    x_block = work.at[pl.ds(rows, rows)]
    gram_t(work.at[pl.ds(0, rows)], x_block, rows)
    g_ref[1] = oriented(acc[pl.ds(0, rows), :], 1)

    stores = []
    for i in range(BATCHES):
        fwd_right[i].wait_recv()
        fwd_left[i].wait_recv()
        far_relay[i].start()
        gram_t(far.at[i, pl.ds(0, 2 * piece)], x_block, 2 * piece)
        for s in (0, 1):
            x_gram[pl.ds(s * half + i * piece, piece), :] = acc[pl.ds(s * piece, piece), :]
        far_relay[i].wait_recv()
        gram_t(far.at[i], own, 4 * piece)
        for s in (0, 1):
            part = acc[pl.ds(s * piece, piece), :]
            g_ref[4, pl.ds(s * half + i * piece, piece), :] = jnp.where(me >= groups // 2, 0.0, part)
        if i < BATCHES - 1:
            apply(far.at[i], 4 * piece)
        else:
            coef = acc[pl.ds(0, 4 * piece), :].astype(jnp.bfloat16).T
            width = cols // OUT_PARTS
            for part in range(OUT_PARTS):
                for sub in range(width // APPLY_STEP):
                    sl = pl.ds(part * width + sub * APPLY_STEP, APPLY_STEP)
                    y_acc[:, sl] += jnp.dot(coef, far[i, :, sl], preferred_element_type=jnp.float32)
                sl = pl.ds(part * width, width)
                copy = pltpu.make_async_copy(y_acc.at[:, sl], y_ref.at[:, sl], out_sem.at[part])
                copy.start()
                stores.append(copy)
    g_ref[3] = oriented(x_gram[...], 3)
    for copy in stores:
        copy.wait()
    for copy in to_right + to_left + [to_sib] + fwd_right + fwd_left + relay[0] + relay[1] + far_relay:
        copy.wait_send()


def solution(mesh):
    groups = mesh.shape["row"]

    def per_device(own_block):
        rows, cols = own_block.shape
        slots = groups // 2 + 1
        far_rows = 2 * rows // BATCHES
        dma = pltpu.SemaphoreType.DMA
        y, gram, _ = pl.pallas_call(
            functools.partial(kernel, groups),
            out_shape=(
                jax.ShapeDtypeStruct((rows, cols), jnp.float32),
                jax.ShapeDtypeStruct((slots, rows, rows), jnp.float32),
                jax.ShapeDtypeStruct((5, rows, cols), jnp.bfloat16),
            ),
            in_specs=[pl.BlockSpec(memory_space=pl.ANY)],
            out_specs=(
                pl.BlockSpec(memory_space=pl.ANY),
                pl.BlockSpec(memory_space=pltpu.VMEM),
                pl.BlockSpec(memory_space=pl.ANY),
            ),
            scratch_shapes=[
                pltpu.VMEM((rows, cols), jnp.bfloat16),
                pltpu.VMEM((2 * rows, cols), jnp.bfloat16),
                pltpu.VMEM((BATCHES, far_rows, cols), jnp.bfloat16),
                pltpu.VMEM((2 * rows, rows), jnp.float32),
                pltpu.VMEM((rows, cols), jnp.float32),
                pltpu.VMEM((rows, rows), jnp.float32),
                dma((5,)), dma((5,)),
                dma((2 * BATCHES,)), dma((2 * BATCHES,)),
                dma((4,)), dma((4,)),
                dma((BATCHES,)), dma((BATCHES,)),
                dma((7,)), dma((OUT_PARTS,)),
            ],
            compiler_params=pltpu.CompilerParams(
                collective_id=0, has_side_effects=True, vmem_limit_bytes=VMEM_LIMIT),
        )(own_block)
        return gram[None], y

    return jax.shard_map(
        per_device, mesh=mesh, in_specs=(P(("mat", "row"), None),),
        out_specs=(P(("mat", "row"), None, None, None), P(("mat", "row"), None)), check_vma=False)
```

time: 1370 us -> 306 us (0.22)
  the two profiles are of different devices: /device:TPU:80 before, /device:TPU:81 now
where the time goes in v1:
time: 306 us
  Pallas kernels  291 us (95%)
  local copies, waits for them, and re-layouts  14 us (5%)
    pallas_call x1, Pallas kernels, per_device(): pl.pallas_call(functools.partial(kernel, groups), out_shape=(jax.ShapeDty...  291 us
    unnamed x2, local copies, waits for them, and re-layouts  14 us

profile of v1, /device:TPU:81, one launch (start us, length us, event | category | flops | bytes accessed | tf_op | source)
XLA Modules:
  0.0 305.6 jit_solution(16375861984085230815)
XLA Ops:
  0.6 291.0 %shard_map.30 = (f32[256,16384]{1,0:T(8,128)}, f32[5,256,256]{2,1,0:T(8,128)}, bf16[5,256,16384]{2,1,0:T(8,128)(2,1)}) custom-call(bf16[256,16384]{1,0:T(8,128)(2,1)} %a_ref.1), custom_call_target="tpu_custom_call" | custom-call | tf_op jit(solution)/shard_map/pallas_call | solution.py:177
  291.6 2.5 copy.5
  294.1 11.5 %copy.6 = f32[256,16384]{1,0:T(8,128)} copy(f32[256,16384]{1,0:T(8,128)} %get-tuple-element.9) | data formatting | bytes 33554432

commit v2 on v1

--- a/solution.py
+++ b/solution.py
@@ -10,15 +10,14 @@
 BATCHES = 4
 GRAM_STEP = 2048
 APPLY_STEP = 1024
-OUT_PARTS = 8
-VMEM_LIMIT = 67043328
+VMEM_LIMIT = 46 << 20
 
 NT = (((1,), (1,)), ((), ()))
 
 
-def kernel(groups, a_ref, y_ref, g_ref, hb, own, work, far, acc, y_acc, x_gram,
+def kernel(groups, a_ref, y_acc, g_ref, hb, own, work, far, acc, x_gram,
            own_send, own_recv, fwd_send, fwd_recv, relay_send, relay_recv,
-           far_send, far_recv, load_sem, out_sem):
+           far_send, far_recv, load_sem):
     rows, cols = a_ref.shape
     half = rows // 2
     piece = half // BATCHES
@@ -133,7 +132,6 @@
     gram_t(work.at[pl.ds(0, rows)], x_block, rows)
     g_ref[1] = oriented(acc[pl.ds(0, rows), :], 1)
 
-    stores = []
     for i in range(BATCHES):
         fwd_right[i].wait_recv()
         fwd_left[i].wait_recv()
@@ -146,22 +144,8 @@
         for s in (0, 1):
             part = acc[pl.ds(s * piece, piece), :]
             g_ref[4, pl.ds(s * half + i * piece, piece), :] = jnp.where(me >= groups // 2, 0.0, part)
-        if i < BATCHES - 1:
-            apply(far.at[i], 4 * piece)
-        else:
-            coef = acc[pl.ds(0, 4 * piece), :].astype(jnp.bfloat16).T
-            width = cols // OUT_PARTS
-            for part in range(OUT_PARTS):
-                for sub in range(width // APPLY_STEP):
-                    sl = pl.ds(part * width + sub * APPLY_STEP, APPLY_STEP)
-                    y_acc[:, sl] += jnp.dot(coef, far[i, :, sl], preferred_element_type=jnp.float32)
-                sl = pl.ds(part * width, width)
-                copy = pltpu.make_async_copy(y_acc.at[:, sl], y_ref.at[:, sl], out_sem.at[part])
-                copy.start()
-                stores.append(copy)
+        apply(far.at[i], 4 * piece)
     g_ref[3] = oriented(x_gram[...], 3)
-    for copy in stores:
-        copy.wait()
     for copy in to_right + to_left + [to_sib] + fwd_right + fwd_left + relay[0] + relay[1] + far_relay:
         copy.wait_send()
 
@@ -177,13 +161,13 @@
         y, gram, _ = pl.pallas_call(
             functools.partial(kernel, groups),
             out_shape=(
-                jax.ShapeDtypeStruct((rows, cols), jnp.float32),
-                jax.ShapeDtypeStruct((slots, rows, rows), jnp.float32),
+                pltpu.VMEM((rows, cols), jnp.float32),
+                pltpu.VMEM((slots, rows, rows), jnp.float32),
                 jax.ShapeDtypeStruct((5, rows, cols), jnp.bfloat16),
             ),
             in_specs=[pl.BlockSpec(memory_space=pl.ANY)],
             out_specs=(
-                pl.BlockSpec(memory_space=pl.ANY),
+                pl.BlockSpec(memory_space=pltpu.VMEM),
                 pl.BlockSpec(memory_space=pltpu.VMEM),
                 pl.BlockSpec(memory_space=pl.ANY),
             ),
@@ -192,13 +176,12 @@
                 pltpu.VMEM((2 * rows, cols), jnp.bfloat16),
                 pltpu.VMEM((BATCHES, far_rows, cols), jnp.bfloat16),
                 pltpu.VMEM((2 * rows, rows), jnp.float32),
-                pltpu.VMEM((rows, cols), jnp.float32),
                 pltpu.VMEM((rows, rows), jnp.float32),
                 dma((5,)), dma((5,)),
                 dma((2 * BATCHES,)), dma((2 * BATCHES,)),
                 dma((4,)), dma((4,)),
                 dma((BATCHES,)), dma((BATCHES,)),
-                dma((7,)), dma((OUT_PARTS,)),
+                dma((7,)),
             ],
             compiler_params=pltpu.CompilerParams(
                 collective_id=0, has_side_effects=True, vmem_limit_bytes=VMEM_LIMIT),

time: 306 us -> 297 us (0.971)
  local copies, waits for them, and re-layouts: 14 us -> 7.22 us
    unnamed x2, local copies, waits for them, and re-layouts: 14 us -> 7.22 us
where the time goes in v2:
time: 297 us; the launch traced here: 296 us
  Pallas kernels  288 us (97%)
  local copies, waits for them, and re-layouts  7.22 us (2%)
    pallas_call x1, Pallas kernels, per_device(): pl.pallas_call(functools.partial(kernel, groups), out_shape=(pltpu.VMEM((...  288 us
    unnamed x2, local copies, waits for them, and re-layouts  7.22 us

profile of v2, /device:TPU:81, one launch (start us, length us, event | category | flops | bytes accessed | tf_op | source)
XLA Modules:
  0.0 296.3 jit_solution(4781451754353612664)
XLA Ops:
  0.6 288.5 %shard_map.30 = (f32[256,16384]{1,0:T(8,128)S(1)}, f32[5,256,256]{2,1,0:T(8,128)S(1)}, bf16[5,256,16384]{2,1,0:T(8,128)(2,1)}) custom-call(bf16[256,16384]{1,0:T(8,128)(2,1)} %a_ref.1), custom_call_target="tpu_custom_call" | custom-call | tf_op jit(solution)/shard_map/pallas_call | solution.py:161
  289.1 1.1 copy.5
  290.2 6.2 %copy.6 = f32[256,16384]{1,0:T(8,128)} copy(f32[256,16384]{1,0:T(8,128)S(1)} %get-tuple-element.7) | data formatting | bytes 33554432

commit v3 on v2

v3 whole, which is shorter than its diff:
```python
import functools

import jax
import jax.numpy as jnp
from jax import lax
from jax.experimental import pallas as pl
from jax.experimental.pallas import tpu as pltpu
from jax.sharding import PartitionSpec as P

GRAM_STEP = 4096
APPLY_STEP = 2048
LAST_CHUNKS = 8
OUT_PARTS = 16
GATHER_VMEM = 40 << 20
FINISH_VMEM = 18 << 20

NT = (((1,), (1,)), ((), ()))


def piece_rows(half):
    return (half // 2, half // 4), half // 4


def oriented(me, groups, value, slot):
    first_blk = lax.rem(me + slot % 2, groups)
    return jnp.where(first_blk + slot >= groups, value.T, value)


def gather_kernel(groups, a_ref, y_ref, g_ref, tail_gram, tail, hb, own, work, far, acc,
                  own_send, own_recv, fwd_send, fwd_recv, relay_send, relay_recv,
                  far_send, far_recv, last_send, last_recv, tail_send, tail_recv, load_sem):
    rows, cols = a_ref.shape
    half = rows // 2
    early, late = piece_rows(half)
    me = lax.axis_index("row")
    core = lax.rem(me, 2)
    right = lax.rem(me + 2, groups)
    left = lax.rem(me + groups - 2, groups)
    sib = me + 1 - 2 * core

    def remote(src, dst, send, recv, to):
        return pltpu.make_async_remote_copy(
            src_ref=src, dst_ref=dst, send_sem=send, recv_sem=recv,
            device_id={"row": to}, device_id_type=pl.DeviceIdType.MESH)

    barrier = pltpu.get_barrier_semaphore()
    for peer in (left, right, sib):
        pl.semaphore_signal(barrier, inc=1, device_id={"row": peer}, device_id_type=pl.DeviceIdType.MESH)
    pl.semaphore_wait(barrier, 3)

    def half_rows(index):
        return pl.ds(index * half, half)

    to_right = [remote(a_ref.at[half_rows(s)], hb.at[1, half_rows(s)], own_send.at[s], own_recv.at[s], right) for s in (0, 1)]
    to_left = [remote(a_ref.at[half_rows(s)], hb.at[2, half_rows(s)], own_send.at[2 + s], own_recv.at[2 + s], left) for s in (0, 1)]
    to_sib = remote(a_ref, hb.at[0], own_send.at[4], own_recv.at[4], sib)
    to_right[0].start()
    to_left[1].start()
    to_right[1].start()
    to_left[0].start()
    to_sib.start()

    fwd, far_relay, batch, offset = [], [], [], 0
    for i, piece in enumerate(early):
        base = 4 * offset
        batch.append(far.at[pl.ds(base, 4 * piece)])
        fwd.append([remote(hb.at[1 + side, pl.ds(side * half + offset, piece)], far.at[pl.ds(base + side * piece, piece)],
                           fwd_send.at[2 * i + side], fwd_recv.at[2 * i + side], (right, left)[side]) for side in (0, 1)])
        far_relay.append(remote(far.at[pl.ds(base, 2 * piece)], far.at[pl.ds(base + 2 * piece, 2 * piece)],
                                far_send.at[i], far_recv.at[i], sib))
        offset += piece
    late_offset = offset
    width = cols // LAST_CHUNKS
    last, tail_relay = [], []
    for q in range(LAST_CHUNKS):
        sl = pl.ds(q * width, width)
        last.append([remote(hb.at[1 + side, pl.ds(side * half + late_offset, late), sl], tail.at[pl.ds(side * late, late), sl],
                            last_send.at[2 * q + side], last_recv.at[2 * q + side], (right, left)[side]) for side in (0, 1)])
        tail_relay.append(remote(tail.at[pl.ds(0, 2 * late), sl], tail.at[pl.ds(2 * late, 2 * late), sl],
                                 tail_send.at[q], tail_recv.at[q], sib))
    relay = [[remote(hb.at[1 + side, half_rows(s)], hb.at[3 + side, half_rows(s)],
                     relay_send.at[2 * side + s], relay_recv.at[2 * side + s], sib) for s in (0, 1)] for side in (0, 1)]

    def gram_t(left_ref, right_ref, count):
        acc[pl.ds(0, count), :] = jnp.zeros((count, rows), jnp.float32)

        def body(step, carry):
            sl = pl.ds(pl.multiple_of(step * GRAM_STEP, GRAM_STEP), GRAM_STEP)
            acc[pl.ds(0, count), :] += lax.dot_general(
                left_ref[:, sl], right_ref[:, sl], NT, preferred_element_type=jnp.float32)
            return carry

        lax.fori_loop(0, cols // GRAM_STEP, body, 0)

    def apply(b_ref, count, first=False):
        coef = acc[pl.ds(0, count), :].astype(jnp.bfloat16).T

        def body(step, carry):
            sl = pl.ds(pl.multiple_of(step * APPLY_STEP, APPLY_STEP), APPLY_STEP)
            term = jnp.dot(coef, b_ref[:, sl], preferred_element_type=jnp.float32)
            y_ref[:, sl] = term if first else y_ref[:, sl] + term
            return carry

        lax.fori_loop(0, cols // APPLY_STEP, body, 0)

    def load(src, dst, sem):
        copy = pltpu.make_async_copy(src, dst, sem)
        copy.start()
        return copy

    lower, upper = work.at[pl.ds(0, rows)], work.at[pl.ds(rows, rows)]
    load(a_ref, own, load_sem.at[0]).wait()
    gram_t(own, own, rows)
    g_ref[0] = acc[pl.ds(0, rows), :]
    apply(own, rows, first=True)

    to_sib.wait_recv()
    load(hb.at[0], lower, load_sem.at[1]).wait()
    gram_t(lower, own, rows)
    apply(lower, rows)

    for turn in (0, 1):
        arrivals = (to_right[turn], to_left[1 - turn])
        for copy in arrivals:
            copy.wait_recv()
        if turn == 0:
            for pair in fwd + last:
                for copy in pair:
                    copy.start()
        picks = (relay[0][turn], relay[1][1 - turn])
        for copy in picks:
            copy.start()
        halves = (half_rows(turn), half_rows(1 - turn))
        loads = [load(hb.at[1 + side, halves[side]], work.at[half_rows(side)], load_sem.at[2 + 4 * turn + side]) for side in (0, 1)]
        for side, copy in enumerate(picks):
            copy.wait_recv()
            loads.append(load(hb.at[3 + side, halves[side]], work.at[half_rows(2 + side)], load_sem.at[4 + 4 * turn + side]))
        for copy in loads:
            copy.wait()
        gram_t(work, own, 2 * rows)
        g_ref[2, halves[1], :] = acc[half_rows(1), :]
        apply(work, 2 * rows)
    g_ref[2] = oriented(me, groups, g_ref[2], 2)

    pair_loads = [load(hb.at[2], lower, load_sem.at[10]), load(hb.at[4 * core], upper, load_sem.at[11])]

    def keep_slot(value, row, count):
        g_ref[4, pl.ds(row, count), :] = jnp.where(me >= groups // 2, 0.0, value)

    def next_gram(piece, offset):
        gram_t(far.at[pl.ds(4 * offset, 2 * piece)], upper, 2 * piece)
        for s in (0, 1):
            g_ref[3, pl.ds(s * half + offset, piece), :] = acc[pl.ds(s * piece, piece), :]

    offset = 0
    for i, piece in enumerate(early):
        for copy in fwd[i]:
            copy.wait_recv()
        far_relay[i].start()
        if i > 0:
            next_gram(piece, offset)
        far_relay[i].wait_recv()
        gram_t(batch[i], own, 4 * piece)
        for s in (0, 1):
            keep_slot(acc[pl.ds(s * piece, piece), :], s * half + offset, piece)
        apply(batch[i], 4 * piece)
        if i == 0:
            for copy in pair_loads:
                copy.wait()
            gram_t(lower, upper, rows)
            g_ref[1] = oriented(me, groups, acc[pl.ds(0, rows), :], 1)
            next_gram(piece, offset)
        offset += piece

    near_rows, relay_rows = pl.ds(0, 2 * late), pl.ds(2 * late, 2 * late)

    def add(target, where, q, right_ref):
        sl = pl.ds(q * width, width)
        value = lax.dot_general(tail[where, sl], right_ref[:, sl], NT, preferred_element_type=jnp.float32)
        target[where, :] = value if q == 0 else target[where, :] + value

    for q in range(LAST_CHUNKS + 1):
        if q < LAST_CHUNKS:
            for copy in last[q]:
                copy.wait_recv()
            tail_relay[q].start()
            add(tail_gram, near_rows, q, own)
            add(acc, near_rows, q, upper)
        if q > 0:
            tail_relay[q - 1].wait_recv()
            add(tail_gram, relay_rows, q - 1, own)
    for s in (0, 1):
        g_ref[3, pl.ds(s * half + late_offset, late), :] = acc[pl.ds(s * late, late), :]
        keep_slot(tail_gram[pl.ds(s * late, late), :], s * half + late_offset, late)

    sent = to_right + to_left + [to_sib] + relay[0] + relay[1] + far_relay + tail_relay
    for copy in sent + [copy for pair in fwd + last for copy in pair]:
        copy.wait_send()


def finish_kernel(groups, y_ref, g_ref, tail_gram, tail, y_out, g_out, stage, turned, y_sem, g_sem):
    cols = y_ref.shape[1]
    coef = tail_gram[...].astype(jnp.bfloat16).T
    width = cols // OUT_PARTS
    copies = []
    for part in range(OUT_PARTS):
        sl = pl.ds(part * width, width)
        stage[:, sl] = y_ref[:, sl] + jnp.dot(coef, tail[:, sl], preferred_element_type=jnp.float32)
        copy = pltpu.make_async_copy(stage.at[:, sl], y_out.at[:, sl], y_sem.at[part])
        copy.start()
        copies.append(copy)
    turned[...] = oriented(lax.axis_index("row"), groups, g_ref[3], 3)
    for index, (src, slots) in enumerate(((g_ref.at[0:3], slice(0, 3)), (turned, 3), (g_ref.at[4], 4))):
        copy = pltpu.make_async_copy(src, g_out.at[slots], g_sem.at[index])
        copy.start()
        copies.append(copy)
    for copy in copies:
        copy.wait()


def solution(mesh):
    groups = mesh.shape["row"]

    def per_device(own_block):
        rows, cols = own_block.shape
        slots = groups // 2 + 1
        early, late = piece_rows(rows // 2)
        dma = pltpu.SemaphoreType.DMA
        whole = pl.BlockSpec(memory_space=pltpu.VMEM)
        raw = pl.BlockSpec(memory_space=pl.ANY)
        y_part, gram, tail_gram, tail, _ = pl.pallas_call(
            functools.partial(gather_kernel, groups),
            out_shape=(
                pltpu.VMEM((rows, cols), jnp.float32),
                pltpu.VMEM((slots, rows, rows), jnp.float32),
                pltpu.VMEM((4 * late, rows), jnp.float32),
                pltpu.VMEM((4 * late, cols), jnp.bfloat16),
                jax.ShapeDtypeStruct((5, rows, cols), jnp.bfloat16),
            ),
            in_specs=[raw],
            out_specs=(whole, whole, whole, whole, raw),
            scratch_shapes=[
                pltpu.VMEM((rows, cols), jnp.bfloat16),
                pltpu.VMEM((2 * rows, cols), jnp.bfloat16),
                pltpu.VMEM((4 * sum(early), cols), jnp.bfloat16),
                pltpu.VMEM((2 * rows, rows), jnp.float32),
                dma((5,)), dma((5,)),
                dma((2 * len(early),)), dma((2 * len(early),)),
                dma((4,)), dma((4,)),
                dma((len(early),)), dma((len(early),)),
                dma((2 * LAST_CHUNKS,)), dma((2 * LAST_CHUNKS,)),
                dma((LAST_CHUNKS,)), dma((LAST_CHUNKS,)),
                dma((12,)),
            ],
            compiler_params=pltpu.CompilerParams(
                collective_id=0, has_side_effects=True, vmem_limit_bytes=GATHER_VMEM),
        )(own_block)
        applied, gram = pl.pallas_call(
            functools.partial(finish_kernel, groups),
            out_shape=(
                jax.ShapeDtypeStruct((rows, cols), jnp.float32),
                jax.ShapeDtypeStruct((slots, rows, rows), jnp.float32),
            ),
            in_specs=[whole, whole, whole, whole],
            out_specs=(raw, raw),
            scratch_shapes=[pltpu.VMEM((rows, cols), jnp.float32), pltpu.VMEM((rows, rows), jnp.float32), dma((OUT_PARTS,)), dma((3,))],
            compiler_params=pltpu.CompilerParams(vmem_limit_bytes=FINISH_VMEM),
        )(y_part, gram, tail_gram, tail)
        return gram[None], applied

    return jax.shard_map(
        per_device, mesh=mesh, in_specs=(P(("mat", "row"), None),),
        out_specs=(P(("mat", "row"), None, None, None), P(("mat", "row"), None)), check_vma=False)
```

time: 297 us -> 286 us (0.963)
  local copies, waits for them, and re-layouts: 7.22 us -> 0 us
  Pallas kernels: 288 us -> 285 us
    unnamed x2 -> x0, local copies, waits for them, and re-layouts: 7.22 us -> none
    pallas_call x1 -> x2, Pallas kernels: 288 us -> 285 us  [the longest x1 278 us: per_device(): pl.pallas_call(functools.partial(gather_kernel, groups), out_shape=(pltpu...]
where the time goes in v3:
time: 286 us
  Pallas kernels  285 us (100%)
    pallas_call x1, Pallas kernels, per_device(): pl.pallas_call(functools.partial(gather_kernel, groups), out_shape=(pltpu...  278 us
    pallas_call x1, Pallas kernels, per_device(): pl.pallas_call(functools.partial(finish_kernel, groups), out_shape=(jax.S...  6.73 us

profile of v3, /device:TPU:81, one launch (start us, length us, event | category | flops | bytes accessed | tf_op | source)
XLA Modules:
  0.0 285.8 jit_solution(3250430208341339679)
XLA Ops:
  0.6 278.3 %shard_map.30 = (f32[256,16384]{1,0:T(8,128)S(1)}, f32[5,256,256]{2,1,0:T(8,128)S(1)}, f32[128,256]{1,0:T(8,128)S(1)}, bf16[128,16384]{1,0:T(8,128)(2,1)S(1)}, bf16[5,256,16384]{2,1,0:T(8,128)(2,1)}) custom-call(bf16[256,16384]{1,0:T(8,128)(2,1)} %a_ref.1), custom_call_target="tpu_custom_call" | custom-call | tf_op jit(solution)/shard_map/pallas_call | solution.py:231
  278.9 6.7 %shard_map.31 = (f32[256,16384]{1,0:T(8,128)}, f32[5,256,256]{2,1,0:T(8,128)}) custom-call(f32[256,16384]{1,0:T(8,128)S(1)} %get-tuple-element.8.y_ref, f32[5,256,256]{2,1,0:T(8,128)S(1)} %get-tuple-element.9.g_ref, f32[128,256]{1,0:T(8,128)S(1)} %get-tuple-element.10.tail_gram, bf16[128,16384]{1,0:T(8,128)(2,1)S(1)} %get-tuple-element.11.tail), custom_call_target="tpu_custom_call" | custom-call | tf_op jit(solution)/shard_map/pallas_call | solution.py:258

commit v4 on v3

--- a/solution.py
+++ b/solution.py
@@ -192,26 +192,23 @@
     for s in (0, 1):
         g_ref[3, pl.ds(s * half + late_offset, late), :] = acc[pl.ds(s * late, late), :]
         keep_slot(tail_gram[pl.ds(s * late, late), :], s * half + late_offset, late)
+    g_ref[3] = oriented(me, groups, g_ref[3], 3)
 
     sent = to_right + to_left + [to_sib] + relay[0] + relay[1] + far_relay + tail_relay
     for copy in sent + [copy for pair in fwd + last for copy in pair]:
         copy.wait_send()
 
 
-def finish_kernel(groups, y_ref, g_ref, tail_gram, tail, y_out, g_out, stage, turned, y_sem, g_sem):
+def finish_kernel(y_ref, g_ref, tail_gram, tail, y_out, g_out, stage, y_sem, g_sem):
     cols = y_ref.shape[1]
+    copies = [pltpu.make_async_copy(g_ref, g_out, g_sem)]
+    copies[0].start()
     coef = tail_gram[...].astype(jnp.bfloat16).T
     width = cols // OUT_PARTS
-    copies = []
     for part in range(OUT_PARTS):
         sl = pl.ds(part * width, width)
         stage[:, sl] = y_ref[:, sl] + jnp.dot(coef, tail[:, sl], preferred_element_type=jnp.float32)
         copy = pltpu.make_async_copy(stage.at[:, sl], y_out.at[:, sl], y_sem.at[part])
-        copy.start()
-        copies.append(copy)
-    turned[...] = oriented(lax.axis_index("row"), groups, g_ref[3], 3)
-    for index, (src, slots) in enumerate(((g_ref.at[0:3], slice(0, 3)), (turned, 3), (g_ref.at[4], 4))):
-        copy = pltpu.make_async_copy(src, g_out.at[slots], g_sem.at[index])
         copy.start()
         copies.append(copy)
     for copy in copies:
@@ -256,14 +253,14 @@
                 collective_id=0, has_side_effects=True, vmem_limit_bytes=GATHER_VMEM),
         )(own_block)
         applied, gram = pl.pallas_call(
-            functools.partial(finish_kernel, groups),
+            finish_kernel,
             out_shape=(
                 jax.ShapeDtypeStruct((rows, cols), jnp.float32),
                 jax.ShapeDtypeStruct((slots, rows, rows), jnp.float32),
             ),
             in_specs=[whole, whole, whole, whole],
             out_specs=(raw, raw),
-            scratch_shapes=[pltpu.VMEM((rows, cols), jnp.float32), pltpu.VMEM((rows, rows), jnp.float32), dma((OUT_PARTS,)), dma((3,))],
+            scratch_shapes=[pltpu.VMEM((rows, cols), jnp.float32), dma((OUT_PARTS,)), dma],
             compiler_params=pltpu.CompilerParams(vmem_limit_bytes=FINISH_VMEM),
         )(y_part, gram, tail_gram, tail)
         return gram[None], applied

time: 286 us -> 286 us (level)
  no operation moved by 1% of the time
where the time goes in v4:
time: 286 us; the launch traced here: 285 us
  Pallas kernels  285 us (100%)
    pallas_call x1, Pallas kernels, per_device(): pl.pallas_call(functools.partial(gather_kernel, groups), out_shape=(pltpu...  278 us
    pallas_call x1, Pallas kernels, per_device(): pl.pallas_call(finish_kernel, out_shape=(jax.ShapeDtypeStruct((rows, cols...  6.38 us

profile of v4, /device:TPU:81, one launch (start us, length us, event | category | flops | bytes accessed | tf_op | source)
XLA Modules:
  0.0 285.4 jit_solution(13164795624081641304)
XLA Ops:
  0.6 278.3 %shard_map.30 = (f32[256,16384]{1,0:T(8,128)S(1)}, f32[5,256,256]{2,1,0:T(8,128)S(1)}, f32[128,256]{1,0:T(8,128)S(1)}, bf16[128,16384]{1,0:T(8,128)(2,1)S(1)}, bf16[5,256,16384]{2,1,0:T(8,128)(2,1)}) custom-call(bf16[256,16384]{1,0:T(8,128)(2,1)} %a_ref.1), custom_call_target="tpu_custom_call" | custom-call | tf_op jit(solution)/shard_map/pallas_call | solution.py:228
  278.9 6.4 %shard_map.31 = (f32[256,16384]{1,0:T(8,128)}, f32[5,256,256]{2,1,0:T(8,128)}) custom-call(f32[256,16384]{1,0:T(8,128)S(1)} %get-tuple-element.8.y_ref, f32[5,256,256]{2,1,0:T(8,128)S(1)} %get-tuple-element.9.g_ref, f32[128,256]{1,0:T(8,128)S(1)} %get-tuple-element.10.tail_gram, bf16[128,16384]{1,0:T(8,128)(2,1)S(1)} %get-tuple-element.11.tail), custom_call_target="tpu_custom_call" | custom-call | tf_op jit(solution)/shard_map/pallas_call | solution.py:255

commit v5 on v4

--- a/solution.py
+++ b/solution.py
@@ -9,7 +9,8 @@
 
 GRAM_STEP = 4096
 APPLY_STEP = 2048
-LAST_CHUNKS = 8
+LAST_PARTS = (4, 4, 4, 4, 4, 4, 2, 4, 2)
+LEADS = 2
 OUT_PARTS = 16
 GATHER_VMEM = 40 << 20
 FINISH_VMEM = 18 << 20
@@ -28,7 +29,7 @@
 
 def gather_kernel(groups, a_ref, y_ref, g_ref, tail_gram, tail, hb, own, work, far, acc,
                   own_send, own_recv, fwd_send, fwd_recv, relay_send, relay_recv,
-                  far_send, far_recv, last_send, last_recv, tail_send, tail_recv, load_sem):
+                  far_send, far_recv, last_send, last_recv, tail_send, tail_recv, lead_send, lead_recv, load_sem):
     rows, cols = a_ref.shape
     half = rows // 2
     early, late = piece_rows(half)
@@ -70,14 +71,22 @@
                                 far_send.at[i], far_recv.at[i], sib))
         offset += piece
     late_offset = offset
-    width = cols // LAST_CHUNKS
+    count, unit = len(LAST_PARTS), cols // sum(LAST_PARTS)
+    spans = [pl.ds(sum(LAST_PARTS[:q]) * unit, LAST_PARTS[q] * unit) for q in range(count)]
     last, tail_relay = [], []
-    for q in range(LAST_CHUNKS):
-        sl = pl.ds(q * width, width)
+    shared = count - LEADS
+    for q, sl in enumerate(spans[:shared]):
         last.append([remote(hb.at[1 + side, pl.ds(side * half + late_offset, late), sl], tail.at[pl.ds(side * late, late), sl],
                             last_send.at[2 * q + side], last_recv.at[2 * q + side], (right, left)[side]) for side in (0, 1)])
         tail_relay.append(remote(tail.at[pl.ds(0, 2 * late), sl], tail.at[pl.ds(2 * late, 2 * late), sl],
                                  tail_send.at[q], tail_recv.at[q], sib))
+    lead, lead_relay = [], []
+    for q, sl in enumerate(spans[shared:]):
+        lead.append([remote(hb.at[slot, pl.ds(side * half + late_offset, late), sl], tail.at[pl.ds((slot - 1) * late, late), sl],
+                            lead_send.at[6 * q + slot - 1], lead_recv.at[6 * q + slot - 1], (right, left)[side])
+                     for slot, side in ((1, 0), (2, 1), (3, 0), (4, 1))])
+        lead_relay.append([remote(tail.at[pl.ds(2 * late * i, 2 * late), sl], tail.at[pl.ds(2 * late * (1 - i), 2 * late), sl],
+                                  lead_send.at[6 * q + 4 + i], lead_recv.at[6 * q + 4 + i], sib) for i in (0, 1)])
     relay = [[remote(hb.at[1 + side, half_rows(s)], hb.at[3 + side, half_rows(s)],
                      relay_send.at[2 * side + s], relay_recv.at[2 * side + s], sib) for s in (0, 1)] for side in (0, 1)]
 
@@ -135,6 +144,11 @@
         for side, copy in enumerate(picks):
             copy.wait_recv()
             loads.append(load(hb.at[3 + side, halves[side]], work.at[half_rows(2 + side)], load_sem.at[4 + 4 * turn + side]))
+        if turn == 0:
+            @pl.when(core == 1)
+            def _():
+                for copy in sum(lead, []):
+                    copy.start()
         for copy in loads:
             copy.wait()
         gram_t(work, own, 2 * rows)
@@ -175,20 +189,35 @@
     near_rows, relay_rows = pl.ds(0, 2 * late), pl.ds(2 * late, 2 * late)
 
     def add(target, where, q, right_ref):
-        sl = pl.ds(q * width, width)
+        sl = spans[q]
         value = lax.dot_general(tail[where, sl], right_ref[:, sl], NT, preferred_element_type=jnp.float32)
         target[where, :] = value if q == 0 else target[where, :] + value
 
-    for q in range(LAST_CHUNKS + 1):
-        if q < LAST_CHUNKS:
+    for q in range(count):
+        if q < shared:
             for copy in last[q]:
                 copy.wait_recv()
             tail_relay[q].start()
             add(tail_gram, near_rows, q, own)
             add(acc, near_rows, q, upper)
-        if q > 0:
+        else:
+            @pl.when(core == 1)
+            def _():
+                for copy in lead[q - shared]:
+                    copy.wait_recv()
+                for copy in lead_relay[q - shared]:
+                    copy.start()
+        if 0 < q <= shared:
             tail_relay[q - 1].wait_recv()
             add(tail_gram, relay_rows, q - 1, own)
+        if q >= shared:
+            @pl.when(core == 0)
+            def _():
+                for copy in lead_relay[q - shared]:
+                    copy.wait_recv()
+
+            add(tail_gram, pl.ds(0, 4 * late), q, own)
+            add(acc, near_rows, q, upper)
     for s in (0, 1):
         g_ref[3, pl.ds(s * half + late_offset, late), :] = acc[pl.ds(s * late, late), :]
         keep_slot(tail_gram[pl.ds(s * late, late), :], s * half + late_offset, late)
@@ -197,6 +226,11 @@
     sent = to_right + to_left + [to_sib] + relay[0] + relay[1] + far_relay + tail_relay
     for copy in sent + [copy for pair in fwd + last for copy in pair]:
         copy.wait_send()
+
+    @pl.when(core == 1)
+    def _():
+        for copy in sum(lead + lead_relay, []):
+            copy.wait_send()
 
 
 def finish_kernel(y_ref, g_ref, tail_gram, tail, y_out, g_out, stage, y_sem, g_sem):
@@ -245,8 +279,9 @@
                 dma((2 * len(early),)), dma((2 * len(early),)),
                 dma((4,)), dma((4,)),
                 dma((len(early),)), dma((len(early),)),
-                dma((2 * LAST_CHUNKS,)), dma((2 * LAST_CHUNKS,)),
-                dma((LAST_CHUNKS,)), dma((LAST_CHUNKS,)),
+                dma((2 * len(LAST_PARTS),)), dma((2 * len(LAST_PARTS),)),
+                dma((len(LAST_PARTS),)), dma((len(LAST_PARTS),)),
+                dma((6 * LEADS,)), dma((6 * LEADS,)),
                 dma((12,)),
             ],
             compiler_params=pltpu.CompilerParams(

time: 286 us -> 285 us (level)
  no operation moved by 1% of the time
where the time goes in v5:
time: 285 us; the launch traced here: 284 us
  Pallas kernels  284 us (100%)
    pallas_call x1, Pallas kernels, per_device(): pl.pallas_call(functools.partial(gather_kernel, groups), out_shape=(pltpu...  277 us
    pallas_call x1, Pallas kernels, per_device(): pl.pallas_call(finish_kernel, out_shape=(jax.ShapeDtypeStruct((rows, cols...  6.38 us

profile of v5, /device:TPU:81, one launch (start us, length us, event | category | flops | bytes accessed | tf_op | source)
XLA Modules:
  0.0 284.4 jit_solution(8173089669188768634)
XLA Ops:
  0.6 277.3 %shard_map.30 = (f32[256,16384]{1,0:T(8,128)S(1)}, f32[5,256,256]{2,1,0:T(8,128)S(1)}, f32[128,256]{1,0:T(8,128)S(1)}, bf16[128,16384]{1,0:T(8,128)(2,1)S(1)}, bf16[5,256,16384]{2,1,0:T(8,128)(2,1)}) custom-call(bf16[256,16384]{1,0:T(8,128)(2,1)} %a_ref.1), custom_call_target="tpu_custom_call" | custom-call | tf_op jit(solution)/shard_map/pallas_call | solution.py:262
  277.9 6.4 %shard_map.31 = (f32[256,16384]{1,0:T(8,128)}, f32[5,256,256]{2,1,0:T(8,128)}) custom-call(f32[256,16384]{1,0:T(8,128)S(1)} %get-tuple-element.8.y_ref, f32[5,256,256]{2,1,0:T(8,128)S(1)} %get-tuple-element.9.g_ref, f32[128,256]{1,0:T(8,128)S(1)} %get-tuple-element.10.tail_gram, bf16[128,16384]{1,0:T(8,128)(2,1)S(1)} %get-tuple-element.11.tail), custom_call_target="tpu_custom_call" | custom-call | tf_op jit(solution)/shard_map/pallas_call | solution.py:290

commit v6 on v5

--- a/solution.py
+++ b/solution.py
@@ -203,10 +203,10 @@
         else:
             @pl.when(core == 1)
             def _():
-                for copy in lead[q - shared]:
-                    copy.wait_recv()
-                for copy in lead_relay[q - shared]:
-                    copy.start()
+                for i in (0, 1):
+                    for copy in lead[q - shared][2 * i:2 * i + 2]:
+                        copy.wait_recv()
+                    lead_relay[q - shared][i].start()
         if 0 < q <= shared:
             tail_relay[q - 1].wait_recv()
             add(tail_gram, relay_rows, q - 1, own)

time: 285 us -> 284 us (level)
  no operation moved by 1% of the time
where the time goes in v6:
time: 284 us
  Pallas kernels  283 us (100%)
    pallas_call x1, Pallas kernels, per_device(): pl.pallas_call(functools.partial(gather_kernel, groups), out_shape=(pltpu...  277 us
    pallas_call x1, Pallas kernels, per_device(): pl.pallas_call(finish_kernel, out_shape=(jax.ShapeDtypeStruct((rows, cols...  6.38 us

profile of v6, /device:TPU:81, one launch (start us, length us, event | category | flops | bytes accessed | tf_op | source)
XLA Modules:
  0.0 284.3 jit_solution(10356457067284171832)
XLA Ops:
  0.6 277.1 %shard_map.30 = (f32[256,16384]{1,0:T(8,128)S(1)}, f32[5,256,256]{2,1,0:T(8,128)S(1)}, f32[128,256]{1,0:T(8,128)S(1)}, bf16[128,16384]{1,0:T(8,128)(2,1)S(1)}, bf16[5,256,16384]{2,1,0:T(8,128)(2,1)}) custom-call(bf16[256,16384]{1,0:T(8,128)(2,1)} %a_ref.1), custom_call_target="tpu_custom_call" | custom-call | tf_op jit(solution)/shard_map/pallas_call | solution.py:262
  277.7 6.4 %shard_map.31 = (f32[256,16384]{1,0:T(8,128)}, f32[5,256,256]{2,1,0:T(8,128)}) custom-call(f32[256,16384]{1,0:T(8,128)S(1)} %get-tuple-element.8.y_ref, f32[5,256,256]{2,1,0:T(8,128)S(1)} %get-tuple-element.9.g_ref, f32[128,256]{1,0:T(8,128)S(1)} %get-tuple-element.10.tail_gram, bf16[128,16384]{1,0:T(8,128)(2,1)S(1)} %get-tuple-element.11.tail), custom_call_target="tpu_custom_call" | custom-call | tf_op jit(solution)/shard_map/pallas_call | solution.py:290
